TPU v7x, 32 devices: a whole 2x2x4 slice. The times are simulated.
32 devices in a mesh: dp: 8 (over z, x), mp: 4 (over y, core).
Axes of the slice: x: 2, y: 2, z: 4, core: 2. Of those that a mesh axis runs over, the one named last changes fastest.
Arguments:
- query_rows: bfloat16 [2048, 2048], P('dp', 'mp'), may hold values from -6 to 6
- key_rows: bfloat16 [2048, 512], P('dp', 'mp'), may hold values from -6 to 6
- value_matrix: bfloat16 [2048, 512], P('dp', 'mp'), may hold values from -6 to 6
- out_weight: bfloat16 [2048, 5120], P('mp', 'dp'), may hold values from -0.125 to 0.125
- out_grad: bfloat16 [2048, 5120], P('dp', 'mp'), may hold values from -6 to 6
- doc_lengths: int32 [8, 8], P('dp'), may hold values from 1 to 249, as said below
Outputs:
- layer_out: bfloat16 [2048, 5120], P('dp', 'mp')
- query_grad: bfloat16 [2048, 2048], P('dp', 'mp')
- key_grad: bfloat16 [2048, 512], P('dp', 'mp')
- value_grad: bfloat16 [2048, 512], P('dp', 'mp')
- weight_grad: float32 [2048, 5120], P('mp', 'dp')
Inputs may be any that keep to these rules, and one draw needn't show every extreme that they name: `doc_lengths`: each row holds 8 lengths of 1 or more that sum to 256.
All inputs are finite; a program needn't handle non-finite values.
Results may differ from a plain program's by a relative error of at most 0.014.
Values may be sent and summed in bfloat16 or wider, within the bound.
A program may use at most 64 MiB of HBM per device.

v0:
```python
import functools

import jax
import jax.numpy as jnp
from jax import lax
from jax.experimental import pallas as pl
from jax.experimental.pallas import tpu as pltpu
from jax.sharding import PartitionSpec as P

HEAD_WIDTH = 128
TILE = 128


def local_segments(lengths, row_count):
    segment_ends = jnp.cumsum(lengths)
    positions = jnp.arange(row_count, dtype=jnp.int32)
    return jnp.sum((positions[:, None] >= segment_ends[None, :]).astype(jnp.int32), axis=1)


def to_heads(matrix):
    return matrix.reshape(matrix.shape[0], matrix.shape[1] // HEAD_WIDTH, HEAD_WIDTH).transpose(
        1, 0, 2
    )


def from_heads(tensor):
    return tensor.transpose(1, 0, 2).reshape(tensor.shape[1], tensor.shape[0] * tensor.shape[2])


def attend(queries, key_rows, value_matrix, upstreams, segment):
    head_count, row_count, head_size = queries.shape
    tile_rows = min(TILE, row_count)
    block_count = row_count // tile_rows
    softmax_scale = HEAD_WIDTH ** (-0.5)
    offsets = jnp.arange(tile_rows, dtype=jnp.int32)
    empty_rows = jnp.zeros((tile_rows, head_size), jnp.float32)
    key_sums = [empty_rows] * block_count
    value_sums = [empty_rows] * block_count
    attended_blocks = []
    grad_blocks = []
    for block_index in range(block_count):
        row_start = block_index * tile_rows
        query_tile = queries[:, row_start : row_start + tile_rows]
        upstream_tile = upstreams[:, row_start : row_start + tile_rows]
        query_segment = segment[row_start : row_start + tile_rows]
        active = [
            segment[(column_index + 1) * tile_rows - 1] >= query_segment[0]
            for column_index in range(block_index + 1)
        ]
        score_tiles = []
        for column_index in range(block_index + 1):
            column_start = column_index * tile_rows
            key_tile = key_rows[column_start : column_start + tile_rows]
            key_segment = segment[column_start : column_start + tile_rows]
            allowed = (query_segment[:, None] == key_segment[None, :]) & (
                (row_start + offsets)[:, None] >= (column_start + offsets)[None, :]
            )

            def score_tile(query_tile=query_tile, key_tile=key_tile, allowed=allowed):
                logits = (
                    jnp.einsum(
                        "hid,jd->hij", query_tile, key_tile, preferred_element_type=jnp.float32
                    )
                    * softmax_scale
                )
                return jnp.where(allowed[None], logits, -jnp.inf)

            def masked_tile():
                return jnp.full((head_count, tile_rows, tile_rows), -jnp.inf, jnp.float32)

            score_tiles.append(lax.cond(active[column_index], score_tile, masked_tile))
        logits = jnp.concatenate(score_tiles, axis=-1)
        row_max = jnp.max(logits, axis=-1, keepdims=True)
        exp_terms = jnp.exp(logits - row_max)
        probability = exp_terms / jnp.sum(exp_terms, axis=-1, keepdims=True)
        weights = probability.astype(jnp.bfloat16)
        attended = jnp.zeros((head_count, tile_rows, head_size), jnp.float32)
        grad_tiles = []
        for column_index in range(block_index + 1):
            column_start = column_index * tile_rows
            value_tile = value_matrix[column_start : column_start + tile_rows]
            weight_tile = weights[:, :, column_start : column_start + tile_rows]

            def forward_tile(
                weight_tile=weight_tile, value_tile=value_tile, upstream_tile=upstream_tile
            ):
                return (
                    jnp.einsum(
                        "hij,jd->hid", weight_tile, value_tile, preferred_element_type=jnp.float32
                    ),
                    jnp.einsum(
                        "hid,jd->hij", upstream_tile, value_tile, preferred_element_type=jnp.float32
                    ),
                )

            def empty_pair():
                return (
                    jnp.zeros((head_count, tile_rows, head_size), jnp.float32),
                    jnp.zeros((head_count, tile_rows, tile_rows), jnp.float32),
                )

            contribution, prob_grad_tile = lax.cond(active[column_index], forward_tile, empty_pair)
            attended = attended + contribution
            grad_tiles.append(prob_grad_tile)
        prob_grad = jnp.concatenate(grad_tiles, axis=-1)
        row_delta = jnp.sum(probability * prob_grad, axis=-1, keepdims=True)
        score_grad = (probability * (prob_grad - row_delta) * softmax_scale).astype(jnp.bfloat16)
        query_sum = jnp.zeros((head_count, tile_rows, head_size), jnp.float32)
        for column_index in range(block_index + 1):
            column_start = column_index * tile_rows
            key_tile = key_rows[column_start : column_start + tile_rows]
            score_piece = score_grad[:, :, column_start : column_start + tile_rows]
            weight_tile = weights[:, :, column_start : column_start + tile_rows]

            def backward_tile(
                score_piece=score_piece,
                key_tile=key_tile,
                weight_tile=weight_tile,
                query_tile=query_tile,
                upstream_tile=upstream_tile,
            ):
                return (
                    jnp.einsum(
                        "hij,jd->hid", score_piece, key_tile, preferred_element_type=jnp.float32
                    ),
                    jnp.einsum(
                        "hij,hid->jd", score_piece, query_tile, preferred_element_type=jnp.float32
                    ),
                    jnp.einsum(
                        "hij,hid->jd",
                        weight_tile,
                        upstream_tile,
                        preferred_element_type=jnp.float32,
                    ),
                )

            def empty_triple():
                return (
                    jnp.zeros((head_count, tile_rows, head_size), jnp.float32),
                    empty_rows,
                    empty_rows,
                )

            query_part, key_part, value_part = lax.cond(
                active[column_index], backward_tile, empty_triple
            )
            query_sum = query_sum + query_part
            key_sums[column_index] = key_sums[column_index] + key_part
            value_sums[column_index] = value_sums[column_index] + value_part
        attended_blocks.append(attended.astype(jnp.bfloat16))
        grad_blocks.append(query_sum.astype(jnp.bfloat16))
    return (
        jnp.concatenate(attended_blocks, axis=1),
        jnp.concatenate(grad_blocks, axis=1),
        jnp.concatenate(key_sums, axis=0),
        jnp.concatenate(value_sums, axis=0),
    )


def grad_term(grad_full, attended_heads):
    attended_flat = from_heads(attended_heads)
    return lax.dot_general(
        grad_full, attended_flat, (((0,), (0,)), ((), ())), preferred_element_type=jnp.float32
    )


def per_device(query_rows, key_rows, value_matrix, out_weight, out_grad, doc_lengths):
    row_count = query_rows.shape[0]
    weight_full = lax.all_gather(out_weight, "dp", axis=1, tiled=True)
    grad_full = lax.all_gather(out_grad, "mp", axis=1, tiled=True)
    attn_grad = lax.dot_general(
        grad_full, weight_full, (((1,), (1,)), ((), ())), preferred_element_type=jnp.float32
    ).astype(jnp.bfloat16)
    segment = local_segments(doc_lengths[0], row_count)
    queries = to_heads(query_rows)
    upstreams = to_heads(attn_grad)
    attended, query_grad, key_sum, value_sum = attend(
        queries, key_rows, value_matrix, upstreams, segment
    )
    key_grad = key_sum.astype(jnp.bfloat16)
    value_grad = value_sum.astype(jnp.bfloat16)
    weight_part = lax.psum_scatter(
        grad_term(grad_full, attended), "dp", scatter_dimension=0, tiled=True
    )
    attended_flat = from_heads(attended)
    query_grad = from_heads(query_grad)
    partial_sum = jnp.dot(attended_flat, weight_full, preferred_element_type=jnp.float32).astype(
        jnp.bfloat16
    )
    layer_out = lax.psum_scatter(
        lax.optimization_barrier(partial_sum).astype(jnp.float32).astype(jnp.bfloat16),
        "mp",
        scatter_dimension=1,
        tiled=True,
    )
    return (layer_out, query_grad, key_grad, value_grad, weight_part.T)


def dot(a, b, dims):
    return lax.dot_general(a, b, (dims, ((), ())), preferred_element_type=jnp.float32)


NN = ((1,), (0,))
NT = ((1,), (1,))
TN = ((0,), (0,))


def allowed_pairs(lengths_ref, rows):
    row_at = lax.broadcasted_iota(jnp.int32, (rows, 1), 0)
    column_at = lax.broadcasted_iota(jnp.int32, (1, rows), 1)
    row_segment = jnp.zeros((rows, 1), jnp.int32)
    column_segment = jnp.zeros((1, rows), jnp.int32)
    end = jnp.int32(0)
    for index in range(lengths_ref.shape[1]):
        end = end + lengths_ref[0, index]
        row_segment = row_segment + jnp.where(row_at >= end, 1, 0)
        column_segment = column_segment + jnp.where(column_at >= end, 1, 0)
    return (row_segment == column_segment) & (row_at >= column_at)


def branch_kernel(
    n_dp,
    n_mp,
    lengths_ref,
    query_ref,
    key_ref,
    value_ref,
    weight_ref,
    grad_ref,
    layer_ref,
    query_grad_ref,
    key_grad_ref,
    value_grad_ref,
    weight_grad_ref,
    grads,
    heads_all,
    upstream_part,
    twin_in,
    pair_sum,
    upstream_in,
    layer_part,
    layer_in,
    layer_sum,
    layer_done,
    probs,
    swap_send,
    grad_send,
    grad_recv,
    heads_send,
    heads_recv,
    up_send,
    twin_recv,
    pair_send,
    up_recv,
    part_send,
    part_recv,
    done_send,
    done_recv,
):
    d = lax.axis_index("dp")
    m = lax.axis_index("mp")
    ratio = n_dp // n_mp
    rows = query_ref.shape[0]
    columns = weight_ref.shape[1]
    head_count = query_ref.shape[1] // HEAD_WIDTH
    group_size = query_ref.shape[1] // key_ref.shape[1]
    scale = HEAD_WIDTH ** (-0.5)
    home = lax.div(d, ratio)
    slot = lax.rem(d, ratio)
    keeper = lax.rem(d, n_mp)
    line = n_dp // 2
    spot = lax.div(d, 2)
    side = lax.rem(d, 2)
    twin = 2 * spot + 1 - side
    sibling = 2 * lax.div(m, 2) + 1 - lax.rem(m, 2)

    def remote(source, target, send, recv, dp, mp):
        return pltpu.make_async_remote_copy(
            src_ref=source,
            dst_ref=target,
            send_sem=send,
            recv_sem=recv,
            device_id={"dp": dp, "mp": mp},
            device_id_type=pl.DeviceIdType.MESH,
        )

    def swap(j):
        return remote(
            grad_ref.at[:, pl.ds(j * columns, columns)],
            grads.at[d],
            swap_send.at[j],
            grad_recv.at[d],
            ratio * m + j,
            keeper,
        )

    def swap_here(j):
        return pltpu.make_async_copy(
            grad_ref.at[:, pl.ds(j * columns, columns)], grads.at[d], grad_recv.at[d]
        )

    def stays(j):
        return (keeper == m) & (d == ratio * m + j)

    def summed_here(j):
        return (home == m) & (d == m + n_mp * j)

    for j in range(ratio):
        @pl.when(jnp.logical_not(stays(j)))
        def _(j=j):
            swap(j).start()

        @pl.when(stays(j))
        def _(j=j):
            swap_here(j).start()

    allowed = allowed_pairs(lengths_ref, rows)
    for h in range(head_count):
        kv = h // group_size
        head = slice(h * HEAD_WIDTH, (h + 1) * HEAD_WIDTH)
        kv_head = slice(kv * HEAD_WIDTH, (kv + 1) * HEAD_WIDTH)
        logits = dot(query_ref[:, head], key_ref[:, kv_head], NT) * scale
        logits = jnp.where(allowed, logits, -jnp.inf)
        exp_terms = jnp.exp(logits - jnp.max(logits, axis=1, keepdims=True))
        probability = exp_terms / jnp.sum(exp_terms, axis=1, keepdims=True)
        probs[h] = probability
        heads_all[d, :, head] = dot(
            probability.astype(jnp.bfloat16), value_ref[:, kv_head], NN
        ).astype(jnp.bfloat16)

    def heads_copy(block, way):
        target = (d + 2, d - 2, twin)[way]
        return remote(
            heads_all.at[block],
            heads_all.at[block],
            heads_send.at[block, way],
            heads_recv.at[block],
            target,
            m,
        )

    def heads_pass(distance, started):
        def act(block, way):
            if started:
                heads_copy(block, way).start()
            else:
                heads_copy(block, way).wait_send()

        for way, sign in ((0, -1), (1, 1)):
            block = d + sign * 2 * distance
            origin = spot + sign * distance
            onward = spot - sign

            @pl.when((origin >= 0) & (origin < line))
            def _(block=block, way=way, onward=onward):
                if started and distance > 0:
                    heads_arrival(block).wait_recv()

                @pl.when((onward >= 0) & (onward < line))
                def _():
                    act(block, way)

                if distance > 0:
                    act(block, 2)
        if distance == 0:
            act(d, 2)

    def grad_copy(block, step, mp):
        return remote(
            grads.at[block],
            grads.at[block],
            grad_send.at[lax.div(block, n_mp), step],
            grad_recv.at[block],
            d,
            mp,
        )

    def own_grad(j):
        return [grad_copy(m + n_mp * j, 0, sibling)] + [
            grad_copy(m + n_mp * j, step, lax.rem(m + 2 * step, n_mp))
            for step in range(1, n_mp // 2)
        ]

    def across(j, step):
        return lax.rem(m + n_mp - 2 * step, n_mp) + n_mp * j

    def passed_grad(j, step):
        return grad_copy(across(j, step), n_mp // 2 - 1 + step, sibling)

    def grad_arrival(block):
        return remote(
            grads.at[block], grads.at[block], swap_send.at[0], grad_recv.at[block], d, m
        )

    def heads_arrival(block):
        return remote(
            heads_all.at[block], heads_all.at[block], swap_send.at[0], heads_recv.at[block], d, m
        )

    heads_pass(0, True)
    for j in range(ratio):
        grad_arrival(m + n_mp * j).wait_recv()
        for copy in own_grad(j):
            copy.start()

    def up_copy(block):
        return remote(
            upstream_part.at[block],
            twin_in.at[lax.div(block, 2)],
            up_send.at[block],
            twin_recv.at[lax.div(block, 2)],
            twin,
            m,
        )

    def up_block(block):
        upstream_part[block] = dot(grads[block], weight_ref[...], NT).astype(jnp.bfloat16)

        @pl.when(lax.rem(block, 2) != side)
        def _():
            up_copy(block).start()

    def own_step(index, carry):
        up_block(m + n_mp * index)
        return carry

    lax.fori_loop(0, ratio, own_step, 0)
    for step in range(1, n_mp // 2):
        for j in range(ratio):
            grad_arrival(across(j, step)).wait_recv()
            passed_grad(j, step).start()
    heads_pass(1, True)

    def near_step(index, carry):
        up_block(lax.rem(m + n_mp - 2 * (1 + lax.div(index, ratio)), n_mp) + n_mp * lax.rem(index, ratio))
        return carry

    lax.fori_loop(0, ratio * (n_mp // 2 - 1), near_step, 0)

    def far_step(index, carry):
        block = lax.rem(sibling + n_mp - 2 * lax.div(index, ratio), n_mp) + n_mp * lax.rem(index, ratio)
        grad_arrival(block).wait_recv()
        up_block(block)
        return carry

    lax.fori_loop(0, ratio, far_step, 0)
    for distance in range(2, line):
        heads_pass(distance, True)
    lax.fori_loop(ratio, ratio * (n_mp // 2), far_step, 0)

    def pair_copy(place):
        return remote(
            pair_sum.at[place],
            upstream_in.at[spot],
            pair_send.at[place],
            up_recv.at[spot],
            2 * place + side,
            m,
        )

    def pair_step(index, carry):
        place = lax.rem(spot + 1 + index, line)
        remote(
            twin_in.at[place], twin_in.at[place], swap_send.at[0], twin_recv.at[place], d, m
        ).wait_recv()
        total = (
            upstream_part[2 * place + side].astype(jnp.float32)
            + twin_in[place].astype(jnp.float32)
        ).astype(jnp.bfloat16)

        @pl.when(place == spot)
        def _():
            upstream_in[spot] = total

        @pl.when(place != spot)
        def _():
            pair_sum[place] = total
            pair_copy(place).start()

        return carry

    def part_copy(block):
        return remote(
            layer_part.at[block],
            layer_in.at[m, lax.div(block, n_mp)],
            part_send.at[block],
            part_recv.at[m, lax.div(block, n_mp)],
            d,
            lax.rem(block, n_mp),
        )

    def part_step(index, carry):
        block = lax.rem(lax.rem(d + 2 * index, n_dp) + lax.div(index, line) * (twin - d) + n_dp, n_dp)

        @pl.when(index >= line)
        def _():
            heads_arrival(block).wait_recv()

        partial = dot(heads_all[block], weight_ref[...], NN).astype(jnp.bfloat16)

        @pl.when(lax.rem(block, n_mp) == m)
        def _():
            layer_in[m, lax.div(block, n_mp)] = partial

        @pl.when(lax.rem(block, n_mp) != m)
        def _():
            layer_part[block] = partial
            part_copy(block).start()

        return carry

    lax.fori_loop(0, line, part_step, 0)
    lax.fori_loop(0, line, pair_step, 0)
    lax.fori_loop(line, n_dp, part_step, 0)

    weight_grad_ref[...] = jnp.zeros_like(weight_grad_ref)

    def weight_step(block, carry):
        weight_grad_ref[...] += dot(heads_all[block], grads[block], TN)
        return carry

    lax.fori_loop(0, n_dp, weight_step, 0)

    def part_arrival(source, j):
        return remote(
            layer_in.at[source, j],
            layer_in.at[source, j],
            swap_send.at[0],
            part_recv.at[source, j],
            d,
            m,
        )

    def done_copy(j):
        return remote(
            layer_sum.at[j],
            layer_done.at[slot],
            done_send.at[j],
            done_recv.at[slot],
            m + n_mp * j,
            home,
        )

    for j in range(ratio):
        for step in range(1, n_mp):
            part_arrival(lax.rem(m + step, n_mp), j).wait_recv()
        total = layer_in[0, j].astype(jnp.float32)
        for source in range(1, n_mp):
            total = total + layer_in[source, j].astype(jnp.float32)
        layer_sum[j] = total.astype(jnp.bfloat16)

        @pl.when(jnp.logical_not(summed_here(j)))
        def _(j=j):
            done_copy(j).start()

        @pl.when(summed_here(j))
        def _(j=j):
            layer_done[slot] = layer_sum[j]

    def up_arrival(block):
        return remote(
            upstream_in.at[block], upstream_in.at[block], swap_send.at[0], up_recv.at[block], d, m
        )

    for step in range(1, line):
        up_arrival(lax.rem(spot + step, line)).wait_recv()
    for h in range(head_count):
        kv = h // group_size
        head = slice(h * HEAD_WIDTH, (h + 1) * HEAD_WIDTH)
        kv_head = slice(kv * HEAD_WIDTH, (kv + 1) * HEAD_WIDTH)
        upstream = upstream_in[0, :, head].astype(jnp.float32)
        for block in range(1, line):
            upstream = upstream + upstream_in[block, :, head].astype(jnp.float32)
        upstream = upstream.astype(jnp.bfloat16)
        probability = probs[h]
        prob_grad = dot(upstream, value_ref[:, kv_head], NT)
        row_delta = jnp.sum(probability * prob_grad, axis=1, keepdims=True)
        score_grad = (probability * (prob_grad - row_delta) * scale).astype(jnp.bfloat16)
        query_grad_ref[:, head] = dot(score_grad, key_ref[:, kv_head], NN).astype(jnp.bfloat16)
        key_term = dot(score_grad, query_ref[:, head], TN)
        value_term = dot(probability.astype(jnp.bfloat16), upstream, TN)
        if h % group_size == 0:
            key_sum, value_sum = key_term, value_term
        else:
            key_sum, value_sum = key_sum + key_term, value_sum + value_term
        if h % group_size == group_size - 1:
            key_grad_ref[:, kv_head] = key_sum.astype(jnp.bfloat16)
            value_grad_ref[:, kv_head] = value_sum.astype(jnp.bfloat16)

    for j in range(ratio):
        @pl.when(jnp.logical_not(stays(j)))
        def _(j=j):
            remote(
                layer_done.at[j], layer_done.at[j], swap_send.at[0], done_recv.at[j], d, m
            ).wait_recv()

        layer_ref[:, j * columns : (j + 1) * columns] = layer_done[j]

    for j in range(ratio):
        @pl.when(jnp.logical_not(stays(j)))
        def _(j=j):
            swap(j).wait_send()

        @pl.when(jnp.logical_not(summed_here(j)))
        def _(j=j):
            done_copy(j).wait_send()

        for copy in own_grad(j):
            copy.wait_send()
        for step in range(1, n_mp // 2):
            passed_grad(j, step).wait_send()
    for distance in range(line):
        heads_pass(distance, False)
    for step in range(1, line):
        pair_copy(lax.rem(spot + step, line)).wait_send()

    def drain_step(block, carry):
        @pl.when(lax.rem(block, 2) != side)
        def _():
            up_copy(block).wait_send()

        @pl.when(lax.rem(block, n_mp) != m)
        def _():
            part_copy(block).wait_send()

        return carry

    lax.fori_loop(0, n_dp, drain_step, 0)


def fused(n_dp, n_mp, query_rows, key_rows, value_matrix, out_weight, out_grad, doc_lengths):
    rows, width = query_rows.shape
    columns = out_weight.shape[1]
    ratio = n_dp // n_mp
    vmem = pl.BlockSpec(memory_space=pltpu.VMEM)
    dma = pltpu.SemaphoreType.DMA
    return pl.pallas_call(
        functools.partial(branch_kernel, n_dp, n_mp),
        out_shape=(
            jax.ShapeDtypeStruct(out_grad.shape, jnp.bfloat16),
            jax.ShapeDtypeStruct(query_rows.shape, jnp.bfloat16),
            jax.ShapeDtypeStruct(key_rows.shape, jnp.bfloat16),
            jax.ShapeDtypeStruct(value_matrix.shape, jnp.bfloat16),
            jax.ShapeDtypeStruct(out_weight.shape, jnp.float32),
        ),
        in_specs=[pl.BlockSpec(memory_space=pltpu.SMEM)] + [vmem] * 5,
        out_specs=(vmem,) * 5,
        scratch_shapes=[
            pltpu.VMEM((n_dp, rows, columns), jnp.bfloat16),
            pltpu.VMEM((n_dp, rows, width), jnp.bfloat16),
            pltpu.VMEM((n_dp, rows, width), jnp.bfloat16),
            pltpu.VMEM((n_dp // 2, rows, width), jnp.bfloat16),
            pltpu.VMEM((n_dp // 2, rows, width), jnp.bfloat16),
            pltpu.VMEM((n_dp // 2, rows, width), jnp.bfloat16),
            pltpu.VMEM((n_dp, rows, columns), jnp.bfloat16),
            pltpu.VMEM((n_mp, ratio, rows, columns), jnp.bfloat16),
            pltpu.VMEM((ratio, rows, columns), jnp.bfloat16),
            pltpu.VMEM((ratio, rows, columns), jnp.bfloat16),
            pltpu.VMEM((width // HEAD_WIDTH, rows, rows), jnp.float32),
            dma((ratio,)),
            dma((ratio, n_mp)),
            dma((n_dp,)),
            dma((n_dp, 3)),
            dma((n_dp,)),
            dma((n_dp,)),
            dma((n_dp // 2,)),
            dma((n_dp // 2,)),
            dma((n_dp // 2,)),
            dma((n_dp,)),
            dma((n_mp, ratio)),
            dma((ratio,)),
            dma((ratio,)),
        ],
        compiler_params=pltpu.CompilerParams(
            has_side_effects=True, vmem_limit_bytes=56 * 1024 * 1024
        ),
    )(doc_lengths, query_rows, key_rows, value_matrix, out_weight, out_grad)


def body_of(n_dp, n_mp):
    def body(query_rows, key_rows, value_matrix, out_weight, out_grad, doc_lengths):
        arrays = (query_rows, key_rows, value_matrix, out_weight, out_grad, doc_lengths)
        columns = out_weight.shape[1]
        rows, width = query_rows.shape
        held = 2 * n_dp * rows * (4 * columns + 3 * width)
        if (
            columns % 128 == 0
            and rows % 128 == 0
            and n_dp % n_mp == 0
            and n_mp % 2 == 0
            and columns * (n_dp // n_mp) == out_grad.shape[1]
            and held < 24 * 1024 * 1024
        ):
            return fused(n_dp, n_mp, *arrays)
        return per_device(*arrays)

    return body


def solution(mesh):
    placed = (
        P("dp", "mp"),
        P("dp", "mp"),
        P("dp", "mp"),
        P("mp", "dp"),
        P("dp", "mp"),
        P("dp", None),
    )
    return jax.shard_map(
        body_of(mesh.shape["dp"], mesh.shape["mp"]),
        mesh=mesh,
        in_specs=placed,
        out_specs=(P("dp", "mp"), P("dp", "mp"), P("dp", "mp"), P("dp", "mp"), P("mp", "dp")),
        check_vma=False,
    )
```

profile of v0, /device:TPU:14, one launch (start us, length us, event | category | flops | bytes accessed | tf_op | source)
XLA Modules:
  0.0 127.2 jit_solution(11049831392238074075)
XLA Ops:
  0.6 120.5 %shard_map.101 = (bf16[256,1280]{1,0:T(8,128)(2,1)}, bf16[256,512]{1,0:T(8,128)(2,1)}, bf16[256,128]{1,0:T(8,128)(2,1)}, bf16[256,128]{1,0:T(8,128)(2,1)}, f32[512,640]{1,0:T(8,128)}) custom-call(s32[1,8]{1,0:T(1,128)} %lengths_ref.1, bf16[256,512]{1,0:T(8,128)(2,1)} %query_ref.1, bf16[256,128]{1,0:T(8,128)(2,1)} %key_ref.1, bf16[256,128]{1,0:T(8,128)(2,1)} %value_ref.1, ...), custom_call_target="tpu_custom_call" | custom-call | tf_op jit(solution)/shard_map/pallas_call | solution.py:637
  121.1 0.0 copy-start.2
  121.1 0.0 copy-start.1
  121.1 0.0 copy-start
  121.1 2.1 %copy.16 = bf16[256,1280]{1,0:T(8,128)(2,1)} copy(bf16[256,1280]{1,0:T(8,128)(2,1)} %get-tuple-element.10) | data formatting | bytes 1310720
  123.2 1.7 %copy.17 = bf16[256,512]{1,0:T(8,128)(2,1)} copy(bf16[256,512]{1,0:T(8,128)(2,1)} %get-tuple-element.11) | data formatting | bytes 524288
  124.9 0.0 copy-done.2
  124.9 0.6 copy.18
  125.5 0.0 copy-done.1
  125.5 0.6 copy.19
  126.1 0.0 copy-done
  126.1 1.1 copy.20
Async XLA Ops:
  121.1 3.8 %copy-start.2 = (bf16[256,128]{1,0:T(8,128)(2,1)S(1)}, bf16[256,128]{1,0:T(8,128)(2,1)}, u32[]{:S(2)}) copy-start(bf16[256,128]{1,0:T(8,128)(2,1)} %get-tuple-element.12) | copy-start | bytes 196612
  121.1 4.4 %copy-start.1 = (bf16[256,128]{1,0:T(8,128)(2,1)S(1)}, bf16[256,128]{1,0:T(8,128)(2,1)}, u32[]{:S(2)}) copy-start(bf16[256,128]{1,0:T(8,128)(2,1)} %get-tuple-element.13) | copy-start | bytes 196612
  121.1 5.0 %copy-start = (f32[512,640]{1,0:T(8,128)S(1)}, f32[512,640]{1,0:T(8,128)}, u32[]{:S(2)}) copy-start(f32[512,640]{1,0:T(8,128)} %get-tuple-element.14) | copy-start | bytes 3932164
where the time goes:
time: 127 us
  Pallas kernels  120 us (94%)
  local copies, waits for them, and re-layouts  6.07 us (5%)
    pallas_call x1, Pallas kernels, fused(): pl.pallas_call(functools.partial(branch_kernel, n_dp, n_mp), out_shape=(j...  120 us
    unnamed x11, local copies, waits for them, and re-layouts  6.07 us

commit v1 on v0

v1 whole, which is shorter than its diff:
```python
import functools

import jax
import jax.numpy as jnp
from jax import lax
from jax.experimental import pallas as pl
from jax.experimental.pallas import tpu as pltpu
from jax.sharding import PartitionSpec as P

HEAD_WIDTH = 128
TILE = 128


def local_segments(lengths, row_count):
    segment_ends = jnp.cumsum(lengths)
    positions = jnp.arange(row_count, dtype=jnp.int32)
    return jnp.sum((positions[:, None] >= segment_ends[None, :]).astype(jnp.int32), axis=1)


def to_heads(matrix):
    return matrix.reshape(matrix.shape[0], matrix.shape[1] // HEAD_WIDTH, HEAD_WIDTH).transpose(
        1, 0, 2
    )


def from_heads(tensor):
    return tensor.transpose(1, 0, 2).reshape(tensor.shape[1], tensor.shape[0] * tensor.shape[2])


def attend(queries, key_rows, value_matrix, upstreams, segment):
    head_count, row_count, head_size = queries.shape
    tile_rows = min(TILE, row_count)
    block_count = row_count // tile_rows
    softmax_scale = HEAD_WIDTH ** (-0.5)
    offsets = jnp.arange(tile_rows, dtype=jnp.int32)
    empty_rows = jnp.zeros((tile_rows, head_size), jnp.float32)
    key_sums = [empty_rows] * block_count
    value_sums = [empty_rows] * block_count
    attended_blocks = []
    grad_blocks = []
    for block_index in range(block_count):
        row_start = block_index * tile_rows
        query_tile = queries[:, row_start : row_start + tile_rows]
        upstream_tile = upstreams[:, row_start : row_start + tile_rows]
        query_segment = segment[row_start : row_start + tile_rows]
        active = [
            segment[(column_index + 1) * tile_rows - 1] >= query_segment[0]
            for column_index in range(block_index + 1)
        ]
        score_tiles = []
        for column_index in range(block_index + 1):
            column_start = column_index * tile_rows
            key_tile = key_rows[column_start : column_start + tile_rows]
            key_segment = segment[column_start : column_start + tile_rows]
            allowed = (query_segment[:, None] == key_segment[None, :]) & (
                (row_start + offsets)[:, None] >= (column_start + offsets)[None, :]
            )

            def score_tile(query_tile=query_tile, key_tile=key_tile, allowed=allowed):
                logits = (
                    jnp.einsum(
                        "hid,jd->hij", query_tile, key_tile, preferred_element_type=jnp.float32
                    )
                    * softmax_scale
                )
                return jnp.where(allowed[None], logits, -jnp.inf)

            def masked_tile():
                return jnp.full((head_count, tile_rows, tile_rows), -jnp.inf, jnp.float32)

            score_tiles.append(lax.cond(active[column_index], score_tile, masked_tile))
        logits = jnp.concatenate(score_tiles, axis=-1)
        row_max = jnp.max(logits, axis=-1, keepdims=True)
        exp_terms = jnp.exp(logits - row_max)
        probability = exp_terms / jnp.sum(exp_terms, axis=-1, keepdims=True)
        weights = probability.astype(jnp.bfloat16)
        attended = jnp.zeros((head_count, tile_rows, head_size), jnp.float32)
        grad_tiles = []
        for column_index in range(block_index + 1):
            column_start = column_index * tile_rows
            value_tile = value_matrix[column_start : column_start + tile_rows]
            weight_tile = weights[:, :, column_start : column_start + tile_rows]

            def forward_tile(
                weight_tile=weight_tile, value_tile=value_tile, upstream_tile=upstream_tile
            ):
                return (
                    jnp.einsum(
                        "hij,jd->hid", weight_tile, value_tile, preferred_element_type=jnp.float32
                    ),
                    jnp.einsum(
                        "hid,jd->hij", upstream_tile, value_tile, preferred_element_type=jnp.float32
                    ),
                )

            def empty_pair():
                return (
                    jnp.zeros((head_count, tile_rows, head_size), jnp.float32),
                    jnp.zeros((head_count, tile_rows, tile_rows), jnp.float32),
                )

            contribution, prob_grad_tile = lax.cond(active[column_index], forward_tile, empty_pair)
            attended = attended + contribution
            grad_tiles.append(prob_grad_tile)
        prob_grad = jnp.concatenate(grad_tiles, axis=-1)
        row_delta = jnp.sum(probability * prob_grad, axis=-1, keepdims=True)
        score_grad = (probability * (prob_grad - row_delta) * softmax_scale).astype(jnp.bfloat16)
        query_sum = jnp.zeros((head_count, tile_rows, head_size), jnp.float32)
        for column_index in range(block_index + 1):
            column_start = column_index * tile_rows
            key_tile = key_rows[column_start : column_start + tile_rows]
            score_piece = score_grad[:, :, column_start : column_start + tile_rows]
            weight_tile = weights[:, :, column_start : column_start + tile_rows]

            def backward_tile(
                score_piece=score_piece,
                key_tile=key_tile,
                weight_tile=weight_tile,
                query_tile=query_tile,
                upstream_tile=upstream_tile,
            ):
                return (
                    jnp.einsum(
                        "hij,jd->hid", score_piece, key_tile, preferred_element_type=jnp.float32
                    ),
                    jnp.einsum(
                        "hij,hid->jd", score_piece, query_tile, preferred_element_type=jnp.float32
                    ),
                    jnp.einsum(
                        "hij,hid->jd",
                        weight_tile,
                        upstream_tile,
                        preferred_element_type=jnp.float32,
                    ),
                )

            def empty_triple():
                return (
                    jnp.zeros((head_count, tile_rows, head_size), jnp.float32),
                    empty_rows,
                    empty_rows,
                )

            query_part, key_part, value_part = lax.cond(
                active[column_index], backward_tile, empty_triple
            )
            query_sum = query_sum + query_part
            key_sums[column_index] = key_sums[column_index] + key_part
            value_sums[column_index] = value_sums[column_index] + value_part
        attended_blocks.append(attended.astype(jnp.bfloat16))
        grad_blocks.append(query_sum.astype(jnp.bfloat16))
    return (
        jnp.concatenate(attended_blocks, axis=1),
        jnp.concatenate(grad_blocks, axis=1),
        jnp.concatenate(key_sums, axis=0),
        jnp.concatenate(value_sums, axis=0),
    )


def grad_term(grad_full, attended_heads):
    attended_flat = from_heads(attended_heads)
    return lax.dot_general(
        grad_full, attended_flat, (((0,), (0,)), ((), ())), preferred_element_type=jnp.float32
    )


def per_device(query_rows, key_rows, value_matrix, out_weight, out_grad, doc_lengths):
    row_count = query_rows.shape[0]
    weight_full = lax.all_gather(out_weight, "dp", axis=1, tiled=True)
    grad_full = lax.all_gather(out_grad, "mp", axis=1, tiled=True)
    attn_grad = lax.dot_general(
        grad_full, weight_full, (((1,), (1,)), ((), ())), preferred_element_type=jnp.float32
    ).astype(jnp.bfloat16)
    segment = local_segments(doc_lengths[0], row_count)
    queries = to_heads(query_rows)
    upstreams = to_heads(attn_grad)
    attended, query_grad, key_sum, value_sum = attend(
        queries, key_rows, value_matrix, upstreams, segment
    )
    key_grad = key_sum.astype(jnp.bfloat16)
    value_grad = value_sum.astype(jnp.bfloat16)
    weight_part = lax.psum_scatter(
        grad_term(grad_full, attended), "dp", scatter_dimension=0, tiled=True
    )
    attended_flat = from_heads(attended)
    query_grad = from_heads(query_grad)
    partial_sum = jnp.dot(attended_flat, weight_full, preferred_element_type=jnp.float32).astype(
        jnp.bfloat16
    )
    layer_out = lax.psum_scatter(
        lax.optimization_barrier(partial_sum).astype(jnp.float32).astype(jnp.bfloat16),
        "mp",
        scatter_dimension=1,
        tiled=True,
    )
    return (layer_out, query_grad, key_grad, value_grad, weight_part.T)


def dot(a, b, dims):
    return lax.dot_general(a, b, (dims, ((), ())), preferred_element_type=jnp.float32)


NN = ((1,), (0,))
NT = ((1,), (1,))
TN = ((0,), (0,))


def allowed_pairs(lengths_ref, rows):
    row_at = lax.broadcasted_iota(jnp.int32, (rows, 1), 0)
    column_at = lax.broadcasted_iota(jnp.int32, (1, rows), 1)
    row_segment = jnp.zeros((rows, 1), jnp.int32)
    column_segment = jnp.zeros((1, rows), jnp.int32)
    end = jnp.int32(0)
    for index in range(lengths_ref.shape[1]):
        end = end + lengths_ref[0, index]
        row_segment = row_segment + jnp.where(row_at >= end, 1, 0)
        column_segment = column_segment + jnp.where(column_at >= end, 1, 0)
    return (row_segment == column_segment) & (row_at >= column_at)


def branch_kernel(
    n_dp,
    n_mp,
    lengths_ref,
    query_ref,
    key_ref,
    value_ref,
    weight_ref,
    grad_ref,
    layer_ref,
    query_grad_ref,
    key_grad_ref,
    value_grad_ref,
    weight_grad_ref,
    weight_all,
    grads,
    relay_in,
    heads_all,
    heads_turned,
    up_own,
    up_in,
    up_out,
    layer_part,
    pair_in,
    pair_out,
    tier_in,
    layer_sum,
    layer_in,
    twin_out,
    twin_in,
    probs,
    weight_send,
    weight_recv,
    swap_send,
    relay_send,
    relay_recv,
    grad_recv,
    lift_send,
    side_send,
    side_recv,
    heads_send,
    heads_recv,
    up_send,
    up_recv,
    pair_send,
    pair_recv,
    tier_send,
    tier_recv,
    done_send,
    done_recv,
    twin_send,
    twin_recv,
):
    d = lax.axis_index("dp")
    m = lax.axis_index("mp")
    line = n_dp // 2
    tiers = n_mp // 2
    rows = query_ref.shape[0]
    part = rows // n_mp
    width = query_ref.shape[1]
    columns = weight_ref.shape[1]
    span = grad_ref.shape[1]
    head_count = width // HEAD_WIDTH
    group_size = width // key_ref.shape[1]
    scale = HEAD_WIDTH ** (-0.5)
    spot = lax.div(d, 2)
    side = lax.rem(d, 2)
    twin = d + 1 - 2 * side
    core = lax.rem(m, 2)
    tier = lax.div(m, 2)
    sibling = m + 1 - 2 * core
    place = core * tiers + tier
    own_columns = pl.ds(pl.multiple_of(side * columns, 128), columns)
    twin_columns = pl.ds(pl.multiple_of((1 - side) * columns, 128), columns)
    own_half = pl.ds(core * tiers, tiers)
    sibling_half = pl.ds((1 - core) * tiers, tiers)
    at_home = spot == m

    def remote(source, target, send, recv, dp, mp):
        return pltpu.make_async_remote_copy(
            src_ref=source,
            dst_ref=target,
            send_sem=send,
            recv_sem=recv,
            device_id={"dp": dp, "mp": mp},
            device_id_type=pl.DeviceIdType.MESH,
        )

    def arrival(target, recv):
        return remote(target, target, weight_send.at[0], recv, d, m)

    def turn(index):
        low = 2 * spot < line
        above = line - 1 - spot
        first = jnp.where(low, above, spot)
        early = jnp.where(low, line - 1 - index, index)
        late = jnp.where(low, index - first, line - 1 - (index - first))
        return jnp.where(index >= line - 1, spot, jnp.where(index < first, early, late))

    def quarter(index):
        return grad_ref.at[pl.ds(pl.multiple_of(index * part, part), part), :]

    weight_copy = remote(
        weight_ref, weight_all.at[:, own_columns], weight_send.at[0], weight_recv.at[0], twin, m
    )
    weight_here = pltpu.make_async_copy(
        weight_ref, weight_all.at[:, own_columns], weight_recv.at[1]
    )

    def direct(step, c):
        target = lax.rem(tier + step, tiers)
        index = c * tiers + target
        return remote(
            quarter(index),
            grads.at[spot, index],
            swap_send.at[step, c],
            grad_recv.at[spot, index],
            2 * m + side,
            2 * target + c,
        )

    def stay():
        return pltpu.make_async_copy(quarter(place), grads.at[spot, place], grad_recv.at[spot, place])

    def relay(step, c):
        target = lax.rem(tier + step, tiers)
        return remote(
            quarter(c * tiers + target),
            relay_in.at[step, c],
            swap_send.at[step, c],
            relay_recv.at[step, c],
            d,
            2 * target + core,
        )

    def relay_origin(step):
        return 2 * lax.rem(tier + tiers - step, tiers) + core

    def onward(step, c):
        return remote(
            relay_in.at[step, c],
            grads.at[spot, c * tiers + tier],
            relay_send.at[step, c],
            grad_recv.at[spot, c * tiers + tier],
            2 * relay_origin(step) + side,
            2 * tier + c,
        )

    def swaps(act, local):
        for step in range(1, tiers):
            for c in range(2):
                @pl.when(at_home)
                def _(step=step, c=c):
                    act(direct(step, c))

                @pl.when(jnp.logical_not(at_home))
                def _(step=step, c=c):
                    act(relay(step, c))

        for c in range(2):
            mine = at_home & (core == c)

            @pl.when(mine)
            def _():
                local()

            @pl.when(jnp.logical_not(mine))
            def _(c=c):
                act(direct(0, c))

    swaps(lambda copy: copy.start(), lambda: stay().start())
    weight_copy.start()
    weight_here.start()

    allowed = allowed_pairs(lengths_ref, rows)
    for h in range(head_count):
        kv = h // group_size
        head = slice(h * HEAD_WIDTH, (h + 1) * HEAD_WIDTH)
        kv_head = slice(kv * HEAD_WIDTH, (kv + 1) * HEAD_WIDTH)
        logits = dot(query_ref[:, head], key_ref[:, kv_head], NT) * scale
        logits = jnp.where(allowed, logits, -jnp.inf)
        exp_terms = jnp.exp(logits - jnp.max(logits, axis=1, keepdims=True))
        probability = exp_terms / jnp.sum(exp_terms, axis=1, keepdims=True)
        probs[h] = probability
        heads_all[spot, :, head] = dot(
            probability.astype(jnp.bfloat16), value_ref[:, kv_head], NN
        ).astype(jnp.bfloat16)

    def heads_copy(block, way):
        return remote(
            heads_all.at[block],
            heads_all.at[block],
            heads_send.at[block, way],
            heads_recv.at[block],
            (d + 2, d - 2)[way],
            m,
        )

    def heads_pass(distance, started):
        for way, sign in ((0, -1), (1, 1)):
            block = spot + sign * distance
            target = spot - sign

            @pl.when((block >= 0) & (block < line))
            def _(block=block, way=way, target=target):
                if started and distance > 0:
                    arrival(heads_all.at[block], heads_recv.at[block]).wait_recv()

                @pl.when((target >= 0) & (target < line))
                def _():
                    if started:
                        heads_copy(block, way).start()
                    else:
                        heads_copy(block, way).wait_send()

    heads_pass(0, True)

    for step in range(1, tiers):
        for c in range(2):
            @pl.when(relay_origin(step) != spot)
            def _(step=step, c=c):
                arrival(relay_in.at[step, c], relay_recv.at[step, c]).wait_recv()
                onward(step, c).start()

    def lift(block, step):
        target = lax.rem(tier + step, tiers)
        return remote(
            grads.at[block, place],
            grads.at[block, place],
            lift_send.at[block, step],
            grad_recv.at[block, place],
            d,
            2 * target + core,
        )

    def lift_step(index, carry):
        block = turn(index)
        arrival(grads.at[block, place], grad_recv.at[block, place]).wait_recv()
        for step in range(1, tiers):
            lift(block, step).start()
        return carry

    lax.fori_loop(0, line, lift_step, 0)

    def layer_begin(block):
        layer_part[block] = dot(heads_all[block], weight_all[...], NN).astype(jnp.bfloat16).reshape(
            n_mp, part, span
        )
        pair_copy(block).start()
        turned = heads_all[block].astype(jnp.float32).T.astype(jnp.bfloat16)
        heads_turned[block] = turned

    def pair_copy(block):
        return remote(
            layer_part.at[block, sibling_half],
            pair_in.at[block],
            pair_send.at[block],
            pair_recv.at[block],
            d,
            sibling,
        )

    def tier_copy(block, step):
        target = lax.rem(tier + step, tiers)
        return remote(
            pair_out.at[block, step],
            tier_in.at[block, step],
            tier_send.at[block, step],
            tier_recv.at[block, step],
            d,
            2 * target + core,
        )

    def layer_pair(block):
        arrival(pair_in.at[block], pair_recv.at[block]).wait_recv()
        for step in range(1, tiers):
            target = lax.rem(tier + step, tiers)
            pair_out[block, step] = (
                layer_part[block, core * tiers + target].astype(jnp.float32)
                + pair_in[block, target].astype(jnp.float32)
            ).astype(jnp.bfloat16)
            tier_copy(block, step).start()

    def done_copy(block):
        return remote(
            layer_sum.at[block],
            layer_in.at[place],
            done_send.at[block],
            done_recv.at[place],
            2 * block + side,
            spot,
        )

    def layer_end(block):
        total = layer_part[block, place].astype(jnp.float32) + pair_in[block, tier].astype(
            jnp.float32
        )
        for step in range(1, tiers):
            arrival(tier_in.at[block, step], tier_recv.at[block, step]).wait_recv()
            total = total + tier_in[block, step].astype(jnp.float32)
        total = total.astype(jnp.bfloat16)
        here = at_home & (block == spot)

        @pl.when(here)
        def _():
            layer_in[place] = total

        @pl.when(jnp.logical_not(here))
        def _():
            layer_sum[block] = total
            done_copy(block).start()

    arrival(weight_all.at[:, twin_columns], weight_recv.at[0]).wait_recv()
    weight_here.wait()

    def side_copy(block):
        return remote(
            grads.at[block, own_half],
            grads.at[block, own_half],
            side_send.at[block],
            side_recv.at[block],
            d,
            sibling,
        )

    def layer_step(index, carry):
        layer_begin(turn(index))
        return carry

    lax.fori_loop(line - 1, line, layer_step, 0)
    heads_pass(1, True)

    def side_step(index, carry):
        block = turn(index)
        for step in range(1, tiers):
            from_place = core * tiers + lax.rem(tier + step, tiers)
            arrival(grads.at[block, from_place], grad_recv.at[block, from_place]).wait_recv()
        side_copy(block).start()
        return carry

    lax.fori_loop(0, line, side_step, 0)

    def up_copy(block, way):
        return remote(
            up_out.at[block],
            up_in.at[way, block],
            up_send.at[block],
            up_recv.at[way, block],
            (d + 2, d - 2)[way],
            m,
        )

    def up_block(index, carry):
        block = turn(index)
        arrival(grads.at[block, sibling_half], side_recv.at[block]).wait_recv()
        up_own[block] = dot(grads[block].reshape(rows, span), weight_all[...], NT)
        return carry

    def up_pass(index, started):
        block = turn(index)
        for way, sign in ((0, 1), (1, -1)):
            origin = spot - sign

            @pl.when((block - spot) * sign > 0)
            def _(way=way, origin=origin):
                if started:
                    inner = (origin >= 0) & (origin < line)

                    @pl.when(inner)
                    def _():
                        arrival(up_in.at[way, block], up_recv.at[way, block]).wait_recv()
                        up_out[block] = (
                            up_own[block] + up_in[way, block].astype(jnp.float32)
                        ).astype(jnp.bfloat16)

                    @pl.when(jnp.logical_not(inner))
                    def _():
                        up_out[block] = up_own[block].astype(jnp.bfloat16)

                    up_copy(block, way).start()
                else:
                    up_copy(block, way).wait_send()

    def up_step(index, carry):
        up_block(index, 0)

        @pl.when((spot == 0) | (spot == line - 1))
        def _():
            up_pass(index, True)

        return carry

    lax.fori_loop(0, line - 1, up_step, 0)
    up_block(line - 1, 0)

    def near(distance, act):
        for sign in (-1, 1):
            block = spot + sign * distance

            @pl.when((block >= 0) & (block < line))
            def _(block=block):
                act(block)

    layer_pair(spot)
    near(1, layer_begin)
    for distance in range(2, line):
        @pl.when((spot != 0) & (spot != line - 1))
        def _(distance=distance):
            up_pass(distance - 2, True)

        heads_pass(distance, True)
        near(distance - 1, layer_pair)
        near(distance, layer_begin)

    @pl.when((spot != 0) & (spot != line - 1))
    def _():
        up_pass(line - 2, True)

    near(line - 1, layer_pair)
    layer_end(spot)
    for distance in range(1, line):
        near(distance, layer_end)

    twin_copy = remote(twin_out, twin_in, twin_send.at[0], twin_recv.at[0], twin, m)

    def weight_half(which):
        total = dot(heads_turned[0], grads[0, :, :, which].reshape(rows, columns), NN)
        for block in range(1, line):
            total = total + dot(
                heads_turned[block], grads[block, :, :, which].reshape(rows, columns), NN
            )
        return total

    twin_out[...] = weight_half(twin_columns).astype(jnp.bfloat16)
    twin_copy.start()
    weight_grad_ref[...] = weight_half(own_columns)

    for way, sign in ((0, -1), (1, 1)):
        @pl.when((spot + sign >= 0) & (spot + sign < line))
        def _(way=way):
            arrival(up_in.at[way, spot], up_recv.at[way, spot]).wait_recv()
            up_own[spot] = up_own[spot] + up_in[way, spot].astype(jnp.float32)

    for h in range(head_count):
        kv = h // group_size
        head = slice(h * HEAD_WIDTH, (h + 1) * HEAD_WIDTH)
        kv_head = slice(kv * HEAD_WIDTH, (kv + 1) * HEAD_WIDTH)
        upstream = up_own[spot, :, head].astype(jnp.bfloat16)
        probability = probs[h]
        prob_grad = dot(upstream, value_ref[:, kv_head], NT)
        row_delta = jnp.sum(probability * prob_grad, axis=1, keepdims=True)
        score_grad = (probability * (prob_grad - row_delta) * scale).astype(jnp.bfloat16)
        query_grad_ref[:, head] = dot(score_grad, key_ref[:, kv_head], NN).astype(jnp.bfloat16)
        key_term = dot(score_grad, query_ref[:, head], TN)
        value_term = dot(probability.astype(jnp.bfloat16), upstream, TN)
        if h % group_size == 0:
            key_sum, value_sum = key_term, value_term
        else:
            key_sum, value_sum = key_sum + key_term, value_sum + value_term
        if h % group_size == group_size - 1:
            key_grad_ref[:, kv_head] = key_sum.astype(jnp.bfloat16)
            value_grad_ref[:, kv_head] = value_sum.astype(jnp.bfloat16)

    arrival(twin_in, twin_recv.at[0]).wait_recv()
    weight_grad_ref[...] += twin_in[...].astype(jnp.float32)

    for c in range(2):
        for level in range(tiers):
            @pl.when(jnp.logical_not(at_home & (place == c * tiers + level)))
            def _(index=c * tiers + level):
                arrival(layer_in.at[index], done_recv.at[index]).wait_recv()

    layer_ref[...] = layer_in[...].reshape(rows, span)

    swaps(lambda copy: copy.wait_send(), lambda: None)
    weight_copy.wait_send()
    for step in range(1, tiers):
        for c in range(2):
            @pl.when(relay_origin(step) != spot)
            def _(step=step, c=c):
                onward(step, c).wait_send()

    for distance in range(line - 1):
        heads_pass(distance, False)
    twin_copy.wait_send()

    def drain_step(block, carry):
        side_copy(block).wait_send()
        pair_copy(block).wait_send()
        for step in range(1, tiers):
            lift(block, step).wait_send()
            tier_copy(block, step).wait_send()

        @pl.when(jnp.logical_not(at_home & (block == spot)))
        def _():
            done_copy(block).wait_send()

        @pl.when(block < line - 1)
        def _():
            up_pass(block, False)

        return carry

    lax.fori_loop(0, line, drain_step, 0)


def fused(n_dp, n_mp, query_rows, key_rows, value_matrix, out_weight, out_grad, doc_lengths):
    rows, width = query_rows.shape
    columns = out_weight.shape[1]
    span = out_grad.shape[1]
    line = n_dp // 2
    tiers = n_mp // 2
    part = rows // n_mp
    vmem = pl.BlockSpec(memory_space=pltpu.VMEM)
    anywhere = pl.BlockSpec(memory_space=pl.ANY)
    dma = pltpu.SemaphoreType.DMA
    bf16 = jnp.bfloat16
    return pl.pallas_call(
        functools.partial(branch_kernel, n_dp, n_mp),
        out_shape=(
            jax.ShapeDtypeStruct(out_grad.shape, bf16),
            jax.ShapeDtypeStruct(query_rows.shape, bf16),
            jax.ShapeDtypeStruct(key_rows.shape, bf16),
            jax.ShapeDtypeStruct(value_matrix.shape, bf16),
            jax.ShapeDtypeStruct(out_weight.shape, jnp.float32),
        ),
        in_specs=[pl.BlockSpec(memory_space=pltpu.SMEM)] + [vmem] * 3 + [anywhere] * 2,
        out_specs=(vmem,) * 5,
        scratch_shapes=[
            pltpu.VMEM((width, span), bf16),
            pltpu.VMEM((line, n_mp, part, span), bf16),
            pltpu.VMEM((tiers, 2, part, span), bf16),
            pltpu.VMEM((line, rows, width), bf16),
            pltpu.VMEM((line, width, rows), bf16),
            pltpu.VMEM((line, rows, width), jnp.float32),
            pltpu.VMEM((2, line, rows, width), bf16),
            pltpu.VMEM((line, rows, width), bf16),
            pltpu.VMEM((line, n_mp, part, span), bf16),
            pltpu.VMEM((line, tiers, part, span), bf16),
            pltpu.VMEM((line, tiers, part, span), bf16),
            pltpu.VMEM((line, tiers, part, span), bf16),
            pltpu.VMEM((line, part, span), bf16),
            pltpu.VMEM((n_mp, part, span), bf16),
            pltpu.VMEM((width, columns), bf16),
            pltpu.VMEM((width, columns), bf16),
            pltpu.VMEM((width // HEAD_WIDTH, rows, rows), jnp.float32),
            dma((1,)),
            dma((2,)),
            dma((tiers, 2)),
            dma((tiers, 2)),
            dma((tiers, 2)),
            dma((line, n_mp)),
            dma((line, tiers)),
            dma((line,)),
            dma((line,)),
            dma((line, 2)),
            dma((line,)),
            dma((line,)),
            dma((2, line)),
            dma((line,)),
            dma((line,)),
            dma((line, tiers)),
            dma((line, tiers)),
            dma((line,)),
            dma((n_mp,)),
            dma((1,)),
            dma((1,)),
        ],
        compiler_params=pltpu.CompilerParams(
            has_side_effects=True, vmem_limit_bytes=60 * 1024 * 1024
        ),
    )(doc_lengths, query_rows, key_rows, value_matrix, out_weight, out_grad)


def body_of(n_dp, n_mp):
    def body(query_rows, key_rows, value_matrix, out_weight, out_grad, doc_lengths):
        arrays = (query_rows, key_rows, value_matrix, out_weight, out_grad, doc_lengths)
        columns = out_weight.shape[1]
        rows, width = query_rows.shape
        held = 2 * n_dp * rows * (4 * columns + 3 * width)
        if (
            columns % 128 == 0
            and rows % 128 == 0
            and rows % (16 * n_mp) == 0
            and n_dp == 2 * n_mp
            and n_mp % 2 == 0
            and n_mp > 2
            and 2 * columns == out_grad.shape[1]
            and held < 24 * 1024 * 1024
        ):
            return fused(n_dp, n_mp, *arrays)
        return per_device(*arrays)

    return body


def solution(mesh):
    placed = (
        P("dp", "mp"),
        P("dp", "mp"),
        P("dp", "mp"),
        P("mp", "dp"),
        P("dp", "mp"),
        P("dp", None),
    )
    return jax.shard_map(
        body_of(mesh.shape["dp"], mesh.shape["mp"]),
        mesh=mesh,
        in_specs=placed,
        out_specs=(P("dp", "mp"), P("dp", "mp"), P("dp", "mp"), P("dp", "mp"), P("mp", "dp")),
        check_vma=False,
    )
```

time: 127 us -> 94.6 us (0.74)
  the two profiles are of different devices: /device:TPU:14 before, /device:TPU:13 now
where the time goes in v1:
time: 94.6 us; the launch traced here: 94.4 us
  Pallas kernels  87.6 us (93%)
  local copies, waits for them, and re-layouts  6.07 us (6%)
    pallas_call x1, Pallas kernels, fused(): pl.pallas_call(functools.partial(branch_kernel, n_dp, n_mp), out_shape=(j...  87.6 us
    unnamed x11, local copies, waits for them, and re-layouts  6.07 us

profile of v1, /device:TPU:13, one launch (start us, length us, event | category | flops | bytes accessed | tf_op | source)
XLA Modules:
  0.0 94.4 jit_solution(12274233608747101188)
XLA Ops:
  0.6 87.6 %shard_map.101 = (bf16[256,1280]{1,0:T(8,128)(2,1)}, bf16[256,512]{1,0:T(8,128)(2,1)}, bf16[256,128]{1,0:T(8,128)(2,1)}, bf16[256,128]{1,0:T(8,128)(2,1)}, f32[512,640]{1,0:T(8,128)}) custom-call(s32[1,8]{1,0:T(1,128)} %lengths_ref.1, bf16[256,512]{1,0:T(8,128)(2,1)} %query_ref.1, bf16[256,128]{1,0:T(8,128)(2,1)} %key_ref.1, bf16[256,128]{1,0:T(8,128)(2,1)} %value_ref.1, ...), custom_call_target="tpu_custom_call" | custom-call | tf_op jit(solution)/shard_map/pallas_call | solution.py:738
  88.3 0.0 copy-start.2
  88.3 0.0 copy-start.1
  88.3 0.0 copy-start
  88.3 2.1 %copy.16 = bf16[256,1280]{1,0:T(8,128)(2,1)} copy(bf16[256,1280]{1,0:T(8,128)(2,1)} %get-tuple-element.10) | data formatting | bytes 1310720
  90.4 1.7 %copy.17 = bf16[256,512]{1,0:T(8,128)(2,1)} copy(bf16[256,512]{1,0:T(8,128)(2,1)} %get-tuple-element.11) | data formatting | bytes 524288
  92.0 0.0 copy-done.2
  92.0 0.6 copy.18
  92.7 0.0 copy-done.1
  92.7 0.6 copy.19
  93.3 0.0 copy-done
  93.3 1.1 %copy.20 = f32[512,640]{1,0:T(8,128)} copy(f32[512,640]{1,0:T(8,128)S(1)} %copy-done) | data formatting | bytes 2621440
Async XLA Ops:
  88.3 3.8 %copy-start.2 = (bf16[256,128]{1,0:T(8,128)(2,1)S(1)}, bf16[256,128]{1,0:T(8,128)(2,1)}, u32[]{:S(2)}) copy-start(bf16[256,128]{1,0:T(8,128)(2,1)} %get-tuple-element.12) | copy-start | bytes 196612
  88.3 4.4 %copy-start.1 = (bf16[256,128]{1,0:T(8,128)(2,1)S(1)}, bf16[256,128]{1,0:T(8,128)(2,1)}, u32[]{:S(2)}) copy-start(bf16[256,128]{1,0:T(8,128)(2,1)} %get-tuple-element.13) | copy-start | bytes 196612
  88.3 5.0 %copy-start = (f32[512,640]{1,0:T(8,128)S(1)}, f32[512,640]{1,0:T(8,128)}, u32[]{:S(2)}) copy-start(f32[512,640]{1,0:T(8,128)} %get-tuple-element.14) | copy-start | bytes 3932164

commit v2 on v1

--- a/solution.py
+++ b/solution.py
@@ -315,7 +315,7 @@
         first = jnp.where(low, above, spot)
         early = jnp.where(low, line - 1 - index, index)
         late = jnp.where(low, index - first, line - 1 - (index - first))
-        return jnp.where(index >= line - 1, spot, jnp.where(index < first, early, late))
+        return jnp.where(index < first, early, late)
 
     def quarter(index):
         return grad_ref.at[pl.ds(pl.multiple_of(index * part, part), part), :]
@@ -435,6 +435,34 @@
 
     heads_pass(0, True)
 
+    def lift(block, step):
+        target = lax.rem(tier + step, tiers)
+        return remote(
+            grads.at[block, place],
+            grads.at[block, place],
+            lift_send.at[block, step],
+            grad_recv.at[block, place],
+            d,
+            2 * target + core,
+        )
+
+    def near(distance, act):
+        if distance == 0:
+            act(spot)
+        else:
+            for sign in (-1, 1):
+                block = spot + sign * distance
+
+                @pl.when((block >= 0) & (block < line))
+                def _(block=block):
+                    act(block)
+
+    def lift_begin(block):
+        arrival(grads.at[block, place], grad_recv.at[block, place]).wait_recv()
+        for step in range(1, tiers):
+            lift(block, step).start()
+
+    near(0, lift_begin)
     for step in range(1, tiers):
         for c in range(2):
             @pl.when(relay_origin(step) != spot)
@@ -442,25 +470,10 @@
                 arrival(relay_in.at[step, c], relay_recv.at[step, c]).wait_recv()
                 onward(step, c).start()
 
-    def lift(block, step):
-        target = lax.rem(tier + step, tiers)
-        return remote(
-            grads.at[block, place],
-            grads.at[block, place],
-            lift_send.at[block, step],
-            grad_recv.at[block, place],
-            d,
-            2 * target + core,
-        )
-
-    def lift_step(index, carry):
-        block = turn(index)
-        arrival(grads.at[block, place], grad_recv.at[block, place]).wait_recv()
-        for step in range(1, tiers):
-            lift(block, step).start()
-        return carry
-
-    lax.fori_loop(0, line, lift_step, 0)
+    near(1, lift_begin)
+    heads_pass(1, True)
+    for distance in range(2, line):
+        near(distance, lift_begin)
 
     def layer_begin(block):
         layer_part[block] = dot(heads_all[block], weight_all[...], NN).astype(jnp.bfloat16).reshape(
@@ -530,9 +543,6 @@
             layer_sum[block] = total
             done_copy(block).start()
 
-    arrival(weight_all.at[:, twin_columns], weight_recv.at[0]).wait_recv()
-    weight_here.wait()
-
     def side_copy(block):
         return remote(
             grads.at[block, own_half],
@@ -543,22 +553,11 @@
             sibling,
         )
 
-    def layer_step(index, carry):
-        layer_begin(turn(index))
-        return carry
-
-    lax.fori_loop(line - 1, line, layer_step, 0)
-    heads_pass(1, True)
-
-    def side_step(index, carry):
-        block = turn(index)
+    def side_begin(block):
         for step in range(1, tiers):
             from_place = core * tiers + lax.rem(tier + step, tiers)
             arrival(grads.at[block, from_place], grad_recv.at[block, from_place]).wait_recv()
         side_copy(block).start()
-        return carry
-
-    lax.fori_loop(0, line, side_step, 0)
 
     def up_copy(block, way):
         return remote(
@@ -570,11 +569,9 @@
             m,
         )
 
-    def up_block(index, carry):
-        block = turn(index)
+    def up_block(block):
         arrival(grads.at[block, sibling_half], side_recv.at[block]).wait_recv()
         up_own[block] = dot(grads[block].reshape(rows, span), weight_all[...], NT)
-        return carry
 
     def up_pass(index, started):
         block = turn(index)
@@ -600,46 +597,6 @@
                     up_copy(block, way).start()
                 else:
                     up_copy(block, way).wait_send()
-
-    def up_step(index, carry):
-        up_block(index, 0)
-
-        @pl.when((spot == 0) | (spot == line - 1))
-        def _():
-            up_pass(index, True)
-
-        return carry
-
-    lax.fori_loop(0, line - 1, up_step, 0)
-    up_block(line - 1, 0)
-
-    def near(distance, act):
-        for sign in (-1, 1):
-            block = spot + sign * distance
-
-            @pl.when((block >= 0) & (block < line))
-            def _(block=block):
-                act(block)
-
-    layer_pair(spot)
-    near(1, layer_begin)
-    for distance in range(2, line):
-        @pl.when((spot != 0) & (spot != line - 1))
-        def _(distance=distance):
-            up_pass(distance - 2, True)
-
-        heads_pass(distance, True)
-        near(distance - 1, layer_pair)
-        near(distance, layer_begin)
-
-    @pl.when((spot != 0) & (spot != line - 1))
-    def _():
-        up_pass(line - 2, True)
-
-    near(line - 1, layer_pair)
-    layer_end(spot)
-    for distance in range(1, line):
-        near(distance, layer_end)
 
     twin_copy = remote(twin_out, twin_in, twin_send.at[0], twin_recv.at[0], twin, m)
 
@@ -651,8 +608,52 @@
             )
         return total
 
+    arrival(weight_all.at[:, twin_columns], weight_recv.at[0]).wait_recv()
+    weight_here.wait()
+    layer_begin(spot)
+    near(0, side_begin)
+    near(1, side_begin)
+    near(0, up_block)
+    heads_pass(2, True)
+    for distance in range(2, line):
+        near(distance, side_begin)
+        near(distance - 1, up_block)
+    near(line - 1, up_block)
+    edge = (spot == 0) | (spot == line - 1)
+
+    def up_turn(index):
+        @pl.when(jnp.logical_not(edge))
+        def _():
+            up_pass(index, True)
+
+    def edge_step(index, carry):
+        up_pass(index, True)
+        return carry
+
+    @pl.when(edge)
+    def _():
+        lax.fori_loop(0, line - 1, edge_step, 0)
+
+    near(0, layer_pair)
+    near(1, layer_begin)
+    for distance in range(2, line - 1):
+        near(distance - 1, layer_pair)
+        near(distance, layer_begin)
+        if distance > 2:
+            heads_pass(distance, True)
+    for index in range(line - 2):
+        up_turn(index)
+        if index == 0:
+            heads_pass(line - 1, True)
+            near(line - 2, layer_pair)
+            near(line - 1, layer_begin)
     twin_out[...] = weight_half(twin_columns).astype(jnp.bfloat16)
     twin_copy.start()
+    near(line - 1, layer_pair)
+    near(0, layer_end)
+    up_turn(line - 2)
+    for distance in range(1, line):
+        near(distance, layer_end)
     weight_grad_ref[...] = weight_half(own_columns)
 
     for way, sign in ((0, -1), (1, 1)):
@@ -787,7 +788,7 @@
             dma((1,)),
         ],
         compiler_params=pltpu.CompilerParams(
-            has_side_effects=True, vmem_limit_bytes=60 * 1024 * 1024
+            has_side_effects=True, vmem_limit_bytes=36 * 1024 * 1024
         ),
     )(doc_lengths, query_rows, key_rows, value_matrix, out_weight, out_grad)
 

time: 94.6 us -> 84.5 us (0.89)
  the two profiles are of different devices: /device:TPU:13 before, /device:TPU:6 now
where the time goes in v2:
time: 84.5 us; the launch traced here: 84.2 us
  Pallas kernels  74.2 us (88%)
  local copies, waits for them, and re-layouts  9.3 us (11%)
    pallas_call x1, Pallas kernels, fused(): pl.pallas_call(functools.partial(branch_kernel, n_dp, n_mp), out_shape=(j...  74.2 us
    unnamed x17, local copies, waits for them, and re-layouts  9.3 us

profile of v2, /device:TPU:6, one launch (start us, length us, event | category | flops | bytes accessed | tf_op | source)
XLA Modules:
  0.0 84.2 jit_solution(6806567022271111363)
XLA Ops:
  0.6 0.0 copy-start
  0.6 1.1 %copy-done = bf16[512,640]{1,0:T(8,128)(2,1)S(1)} copy-done((bf16[512,640]{1,0:T(8,128)(2,1)S(1)}, bf16[512,640]{1,0:T(8,128)(2,1)}, u32[]{:S(2)}) %copy-start) | copy-done | bytes 655384
  1.7 0.0 copy-start.1
  1.7 1.1 %copy-done.1 = bf16[256,1280]{1,0:T(8,128)(2,1)S(1)} copy-done((bf16[256,1280]{1,0:T(8,128)(2,1)S(1)}, bf16[256,1280]{1,0:T(8,128)(2,1)}, u32[]{:S(2)}) %copy-start.1) | copy-done | bytes 655384
  2.8 0.0 copy-start.2
  2.8 0.9 %copy-done.2 = bf16[256,512]{1,0:T(8,128)(2,1)S(1)} copy-done((bf16[256,512]{1,0:T(8,128)(2,1)S(1)}, bf16[256,512]{1,0:T(8,128)(2,1)}, u32[]{:S(2)}) %copy-start.2) | copy-done | bytes 262168
  3.8 0.0 copy-start.3
  3.8 0.8 copy-done.3
  4.6 0.0 copy-start.4
  4.6 0.8 copy-done.4
  5.4 0.0 copy-start.5
  5.4 0.7 copy-done.5
  6.1 74.2 %shard_map.101 = (bf16[256,1280]{1,0:T(8,128)(2,1)S(1)}, bf16[256,512]{1,0:T(8,128)(2,1)S(1)}, bf16[256,128]{1,0:T(8,128)(2,1)S(1)}, bf16[256,128]{1,0:T(8,128)(2,1)S(1)}, f32[512,640]{1,0:T(8,128)S(1)}) custom-call(s32[1,8]{1,0:T(1,128)S(1)} %copy-done.5, bf16[256,512]{1,0:T(8,128)(2,1)S(1)} %copy-done.2, bf16[256,128]{1,0:T(8,128)(2,1)S(1)} %copy-done.3, ...), custom_call_target="tpu_custom_call" | custom-call | tf_op jit(solution)/shard_map/pallas_call | solution.py:739
  80.3 0.8 copy.16
  81.2 0.7 copy.17
  81.9 0.6 copy.18
  82.5 0.6 copy.19
  83.1 1.1 %copy.20 = f32[512,640]{1,0:T(8,128)} copy(f32[512,640]{1,0:T(8,128)S(1)} %get-tuple-element.14) | data formatting | bytes 2621440
Async XLA Ops:
  0.6 1.1 %copy-start = (bf16[512,640]{1,0:T(8,128)(2,1)S(1)}, bf16[512,640]{1,0:T(8,128)(2,1)}, u32[]{:S(2)}) copy-start(bf16[512,640]{1,0:T(8,128)(2,1)} %weight_ref.1) | copy-start | bytes 1966084
  1.7 1.1 %copy-start.1 = (bf16[256,1280]{1,0:T(8,128)(2,1)S(1)}, bf16[256,1280]{1,0:T(8,128)(2,1)}, u32[]{:S(2)}) copy-start(bf16[256,1280]{1,0:T(8,128)(2,1)} %grad_ref.1) | copy-start | bytes 1966084
  2.8 0.9 %copy-start.2 = (bf16[256,512]{1,0:T(8,128)(2,1)S(1)}, bf16[256,512]{1,0:T(8,128)(2,1)}, u32[]{:S(2)}) copy-start(bf16[256,512]{1,0:T(8,128)(2,1)} %query_ref.1) | copy-start | bytes 786436
  3.8 0.8 copy-start.3
  4.6 0.8 copy-start.4
  5.4 0.7 copy-start.5

commit v3 on v2

--- a/solution.py
+++ b/solution.py
@@ -221,10 +221,10 @@
 def branch_kernel(
     n_dp,
     n_mp,
-    lengths_ref,
-    query_ref,
-    key_ref,
-    value_ref,
+    lengths_hbm,
+    query_hbm,
+    key_hbm,
+    value_hbm,
     weight_ref,
     grad_ref,
     layer_ref,
@@ -232,6 +232,10 @@
     key_grad_ref,
     value_grad_ref,
     weight_grad_ref,
+    lengths_ref,
+    query_ref,
+    key_ref,
+    value_ref,
     weight_all,
     grads,
     relay_in,
@@ -270,6 +274,7 @@
     done_recv,
     twin_send,
     twin_recv,
+    load_recv,
 ):
     d = lax.axis_index("dp")
     m = lax.axis_index("mp")
@@ -388,9 +393,34 @@
             def _(c=c):
                 act(direct(0, c))
 
-    swaps(lambda copy: copy.start(), lambda: stay().start())
-    weight_copy.start()
+    barrier = pltpu.get_barrier_semaphore()
+
+    def greet(dp, mp):
+        pl.semaphore_signal(
+            barrier, inc=1, device_id={"dp": dp, "mp": mp}, device_id_type=pl.DeviceIdType.MESH
+        )
+
+    greet(twin, m)
+    for step in reversed(range(line)):
+        for other in range(n_mp):
+            if step or other:
+                greet(lax.rem(d + 2 * step, n_dp), lax.rem(m + other, n_mp))
+    loads = [
+        pltpu.make_async_copy(source, target, load_recv.at[index])
+        for index, (source, target) in enumerate(
+            (
+                (lengths_hbm, lengths_ref),
+                (query_hbm, query_ref),
+                (key_hbm, key_ref),
+                (value_hbm, value_ref),
+            )
+        )
+    ]
+    for copy in loads:
+        copy.start()
     weight_here.start()
+    for copy in loads:
+        copy.wait()
 
     allowed = allowed_pairs(lengths_ref, rows)
     for h in range(head_count):
@@ -405,6 +435,10 @@
         heads_all[spot, :, head] = dot(
             probability.astype(jnp.bfloat16), value_ref[:, kv_head], NN
         ).astype(jnp.bfloat16)
+
+    pl.semaphore_wait(barrier, line * n_mp)
+    swaps(lambda copy: copy.start(), lambda: stay().start())
+    weight_copy.start()
 
     def heads_copy(block, way):
         return remote(
@@ -725,6 +759,31 @@
     lax.fori_loop(0, line, drain_step, 0)
 
 
+def finish_kernel(*refs):
+    count = len(refs) // 2
+    sems = refs[-1]
+    copies = [
+        pltpu.make_async_copy(refs[index], refs[count + index], sems.at[index])
+        for index in range(count)
+    ]
+    for copy in copies:
+        copy.start()
+    for copy in copies:
+        copy.wait()
+
+
+def finish(arrays):
+    anywhere = pl.BlockSpec(memory_space=pl.ANY)
+    return pl.pallas_call(
+        finish_kernel,
+        out_shape=tuple(jax.ShapeDtypeStruct(a.shape, a.dtype) for a in arrays),
+        in_specs=[anywhere] * len(arrays),
+        out_specs=(pl.BlockSpec(memory_space=pltpu.HBM),) * len(arrays),
+        scratch_shapes=[pltpu.SemaphoreType.DMA((len(arrays),))],
+        compiler_params=pltpu.CompilerParams(vmem_limit_bytes=1024 * 1024),
+    )(*arrays)
+
+
 def fused(n_dp, n_mp, query_rows, key_rows, value_matrix, out_weight, out_grad, doc_lengths):
     rows, width = query_rows.shape
     columns = out_weight.shape[1]
@@ -733,7 +792,7 @@
     tiers = n_mp // 2
     part = rows // n_mp
     vmem = pl.BlockSpec(memory_space=pltpu.VMEM)
-    anywhere = pl.BlockSpec(memory_space=pl.ANY)
+    hbm = pl.BlockSpec(memory_space=pltpu.HBM)
     dma = pltpu.SemaphoreType.DMA
     bf16 = jnp.bfloat16
     return pl.pallas_call(
@@ -745,9 +804,13 @@
             jax.ShapeDtypeStruct(value_matrix.shape, bf16),
             jax.ShapeDtypeStruct(out_weight.shape, jnp.float32),
         ),
-        in_specs=[pl.BlockSpec(memory_space=pltpu.SMEM)] + [vmem] * 3 + [anywhere] * 2,
+        in_specs=[hbm] * 6,
         out_specs=(vmem,) * 5,
         scratch_shapes=[
+            pltpu.SMEM(doc_lengths.shape, jnp.int32),
+            pltpu.VMEM(query_rows.shape, bf16),
+            pltpu.VMEM(key_rows.shape, bf16),
+            pltpu.VMEM(value_matrix.shape, bf16),
             pltpu.VMEM((width, span), bf16),
             pltpu.VMEM((line, n_mp, part, span), bf16),
             pltpu.VMEM((tiers, 2, part, span), bf16),
@@ -786,11 +849,12 @@
             dma((n_mp,)),
             dma((1,)),
             dma((1,)),
+            dma((4,)),
         ],
         compiler_params=pltpu.CompilerParams(
-            has_side_effects=True, vmem_limit_bytes=36 * 1024 * 1024
+            has_side_effects=True, collective_id=0, vmem_limit_bytes=36 * 1024 * 1024
         ),
-    )(doc_lengths, query_rows, key_rows, value_matrix, out_weight, out_grad)
+    )(*(pltpu.with_memory_space_constraint(a, pltpu.HBM) for a in (doc_lengths, query_rows, key_rows, value_matrix, out_weight, out_grad)))
 
 
 def body_of(n_dp, n_mp):
@@ -809,7 +873,7 @@
             and 2 * columns == out_grad.shape[1]
             and held < 24 * 1024 * 1024
         ):
-            return fused(n_dp, n_mp, *arrays)
+            return finish(fused(n_dp, n_mp, *arrays))
         return per_device(*arrays)
 
     return body

time: 84.5 us -> 73.3 us (0.87)
  local copies, waits for them, and re-layouts: 9.3 us -> 0 us
  Pallas kernels: 74.2 us -> 72.5 us
    unnamed x17 -> x0, local copies, waits for them, and re-layouts: 9.3 us -> none
    pallas_call x1, Pallas kernels: 74.2 us -> 71.1 us  [fused(): pl.pallas_call(functools.partial(branch_kernel, n_dp, n_mp), out_shape=(j...]
    pallas_call x0 -> x1, Pallas kernels: none -> 1.45 us  [finish(): pl.pallas_call(finish_kernel, out_shape=tuple((jax.ShapeDtypeStruct(a.sha...]
where the time goes in v3:
time: 73.3 us; the launch traced here: 73.2 us
  Pallas kernels  72.5 us (99%)
    pallas_call x1, Pallas kernels, fused(): pl.pallas_call(functools.partial(branch_kernel, n_dp, n_mp), out_shape=(j...  71.1 us

profile of v3, /device:TPU:6, one launch (start us, length us, event | category | flops | bytes accessed | tf_op | source)
XLA Modules:
  0.0 73.2 jit_solution(9696470644404462279)
XLA Ops:
  0.6 71.1 %shard_map.101 = (bf16[256,1280]{1,0:T(8,128)(2,1)S(1)}, bf16[256,512]{1,0:T(8,128)(2,1)S(1)}, bf16[256,128]{1,0:T(8,128)(2,1)S(1)}, bf16[256,128]{1,0:T(8,128)(2,1)S(1)}, f32[512,640]{1,0:T(8,128)S(1)}) custom-call(s32[1,8]{1,0:T(1,128)} %lengths_hbm.1, bf16[256,512]{1,0:T(8,128)(2,1)} %query_hbm.1, bf16[256,128]{1,0:T(8,128)(2,1)} %key_hbm.1, ...), custom_call_target="tpu_custom_call" | custom-call | tf_op jit(solution)/shard_map/pallas_call | solution.py:798
  71.7 1.4 %shard_map.102 = (bf16[256,1280]{1,0:T(8,128)(2,1)}, bf16[256,512]{1,0:T(8,128)(2,1)}, bf16[256,128]{1,0:T(8,128)(2,1)}, bf16[256,128]{1,0:T(8,128)(2,1)}, f32[512,640]{1,0:T(8,128)}) custom-call(bf16[256,1280]{1,0:T(8,128)(2,1)S(1)} %get-tuple-element.10.refs_0_, bf16[256,512]{1,0:T(8,128)(2,1)S(1)} %get-tuple-element.11.refs_1_, ...), custom_call_target="tpu_custom_call" | custom-call | tf_op jit(solution)/shard_map/pallas_call | solution.py:777

commit v4 on v3

--- a/solution.py
+++ b/solution.py
@@ -314,14 +314,6 @@
     def arrival(target, recv):
         return remote(target, target, weight_send.at[0], recv, d, m)
 
-    def turn(index):
-        low = 2 * spot < line
-        above = line - 1 - spot
-        first = jnp.where(low, above, spot)
-        early = jnp.where(low, line - 1 - index, index)
-        late = jnp.where(low, index - first, line - 1 - (index - first))
-        return jnp.where(index < first, early, late)
-
     def quarter(index):
         return grad_ref.at[pl.ds(pl.multiple_of(index * part, part), part), :]
 
@@ -593,44 +585,64 @@
             arrival(grads.at[block, from_place], grad_recv.at[block, from_place]).wait_recv()
         side_copy(block).start()
 
-    def up_copy(block, way):
+    middle = line // 2
+    low = spot < middle
+    gate = jnp.where(low, middle - 1, middle)
+    far_gate = jnp.where(low, middle, middle - 1)
+    edge = (spot == 0) | (spot == line - 1)
+
+    def up_final(block):
         return remote(
             up_out.at[block],
-            up_in.at[way, block],
+            up_in.at[1, spot],
             up_send.at[block],
-            up_recv.at[way, block],
-            (d + 2, d - 2)[way],
+            up_recv.at[1, spot],
+            2 * block + side,
+            m,
+        )
+
+    def up_chain(block):
+        return remote(
+            up_out.at[block],
+            up_in.at[0, block],
+            up_send.at[block],
+            up_recv.at[0, block],
+            jnp.where(low, d + 2, d - 2),
             m,
         )
 
     def up_block(block):
         arrival(grads.at[block, sibling_half], side_recv.at[block]).wait_recv()
         up_own[block] = dot(grads[block].reshape(rows, span), weight_all[...], NT)
-
-    def up_pass(index, started):
-        block = turn(index)
-        for way, sign in ((0, 1), (1, -1)):
-            origin = spot - sign
-
-            @pl.when((block - spot) * sign > 0)
-            def _(way=way, origin=origin):
-                if started:
-                    inner = (origin >= 0) & (origin < line)
-
-                    @pl.when(inner)
-                    def _():
-                        arrival(up_in.at[way, block], up_recv.at[way, block]).wait_recv()
-                        up_out[block] = (
-                            up_own[block] + up_in[way, block].astype(jnp.float32)
-                        ).astype(jnp.bfloat16)
-
-                    @pl.when(jnp.logical_not(inner))
-                    def _():
-                        up_out[block] = up_own[block].astype(jnp.bfloat16)
-
-                    up_copy(block, way).start()
-                else:
-                    up_copy(block, way).wait_send()
+        crosses = ((block < middle) != low) & (block != far_gate)
+
+        @pl.when(jnp.logical_not(crosses) & (block != spot))
+        def _():
+            up_out[block] = up_own[block].astype(jnp.bfloat16)
+            up_final(block).start()
+
+        @pl.when(crosses & edge)
+        def _():
+            up_out[block] = up_own[block].astype(jnp.bfloat16)
+            up_chain(block).start()
+
+    def up_gather(index):
+        block = jnp.where(low, middle + index, middle - 1 - index)
+
+        @pl.when(jnp.logical_not(edge))
+        def _():
+            arrival(up_in.at[0, block], up_recv.at[0, block]).wait_recv()
+            up_out[block] = (up_own[block] + up_in[0, block].astype(jnp.float32)).astype(
+                jnp.bfloat16
+            )
+
+            @pl.when(spot == gate)
+            def _():
+                up_final(block).start()
+
+            @pl.when(spot != gate)
+            def _():
+                up_chain(block).start()
 
     twin_copy = remote(twin_out, twin_in, twin_send.at[0], twin_recv.at[0], twin, m)
 
@@ -646,55 +658,54 @@
     weight_here.wait()
     layer_begin(spot)
     near(0, side_begin)
+    layer_pair(spot)
+    near(1, layer_begin)
     near(1, side_begin)
     near(0, up_block)
-    heads_pass(2, True)
-    for distance in range(2, line):
+    near(1, layer_pair)
+    for distance in range(2, line - 1):
+        heads_pass(distance, True)
         near(distance, side_begin)
         near(distance - 1, up_block)
+    near(line - 2, up_block)
+    near(line - 1, side_begin)
     near(line - 1, up_block)
-    edge = (spot == 0) | (spot == line - 1)
-
-    def up_turn(index):
-        @pl.when(jnp.logical_not(edge))
-        def _():
-            up_pass(index, True)
-
-    def edge_step(index, carry):
-        up_pass(index, True)
-        return carry
-
-    @pl.when(edge)
-    def _():
-        lax.fori_loop(0, line - 1, edge_step, 0)
-
-    near(0, layer_pair)
-    near(1, layer_begin)
-    for distance in range(2, line - 1):
-        near(distance - 1, layer_pair)
+    for distance in range(2, line):
+        if distance == line - 1:
+            heads_pass(distance, True)
+        if distance > 2:
+            near(distance - 1, layer_pair)
         near(distance, layer_begin)
-        if distance > 2:
-            heads_pass(distance, True)
-    for index in range(line - 2):
-        up_turn(index)
-        if index == 0:
-            heads_pass(line - 1, True)
-            near(line - 2, layer_pair)
-            near(line - 1, layer_begin)
+    near(line - 1, layer_pair)
+    layer_end(spot)
     twin_out[...] = weight_half(twin_columns).astype(jnp.bfloat16)
     twin_copy.start()
-    near(line - 1, layer_pair)
-    near(0, layer_end)
-    up_turn(line - 2)
-    for distance in range(1, line):
+    near(1, layer_end)
+    for index in range(1, middle):
+        up_gather(index)
+        near(index + 1, layer_end)
+    for distance in range(middle + 1, line):
         near(distance, layer_end)
     weight_grad_ref[...] = weight_half(own_columns)
 
-    for way, sign in ((0, -1), (1, 1)):
-        @pl.when((spot + sign >= 0) & (spot + sign < line))
-        def _(way=way):
-            arrival(up_in.at[way, spot], up_recv.at[way, spot]).wait_recv()
-            up_own[spot] = up_own[spot] + up_in[way, spot].astype(jnp.float32)
+    def up_add(source):
+        arrival(up_in.at[1, source], up_recv.at[1, source]).wait_recv()
+        up_own[spot] = up_own[spot] + up_in[1, source].astype(jnp.float32)
+
+    for index in range(middle):
+        source = jnp.where(low, index, middle + index)
+
+        @pl.when(source != spot)
+        def _(source=source):
+            up_add(source)
+
+    up_add(far_gate)
+    for index in range(middle):
+        source = jnp.where(low, middle + index, index)
+
+        @pl.when((spot == gate) & (source != far_gate))
+        def _(source=source):
+            up_add(source)
 
     for h in range(head_count):
         kv = h // group_size
@@ -750,9 +761,9 @@
         def _():
             done_copy(block).wait_send()
 
-        @pl.when(block < line - 1)
+        @pl.when(block != spot)
         def _():
-            up_pass(block, False)
+            up_final(block).wait_send()
 
         return carry
 

time: 73.3 us -> 70.7 us (0.965)
  Pallas kernels: 72.5 us -> 69.9 us
    pallas_call x1, Pallas kernels: 71.1 us -> 68.5 us  [fused(): pl.pallas_call(functools.partial(branch_kernel, n_dp, n_mp), out_shape=(j...]
where the time goes in v4:
time: 70.7 us; the launch traced here: 70.6 us
  Pallas kernels  69.9 us (99%)
    pallas_call x1, Pallas kernels, fused(): pl.pallas_call(functools.partial(branch_kernel, n_dp, n_mp), out_shape=(j...  68.5 us
    pallas_call x1, Pallas kernels, finish(): pl.pallas_call(finish_kernel, out_shape=tuple((jax.ShapeDtypeStruct(a.sha...  1.45 us

profile of v4, /device:TPU:6, one launch (start us, length us, event | category | flops | bytes accessed | tf_op | source)
XLA Modules:
  0.0 70.6 jit_solution(12508144984462909179)
XLA Ops:
  0.6 68.5 %shard_map.101 = (bf16[256,1280]{1,0:T(8,128)(2,1)S(1)}, bf16[256,512]{1,0:T(8,128)(2,1)S(1)}, bf16[256,128]{1,0:T(8,128)(2,1)S(1)}, bf16[256,128]{1,0:T(8,128)(2,1)S(1)}, f32[512,640]{1,0:T(8,128)S(1)}) custom-call(s32[1,8]{1,0:T(1,128)} %lengths_hbm.1, bf16[256,512]{1,0:T(8,128)(2,1)} %query_hbm.1, bf16[256,128]{1,0:T(8,128)(2,1)} %key_hbm.1, ...), custom_call_target="tpu_custom_call" | custom-call | tf_op jit(solution)/shard_map/pallas_call | solution.py:809
  69.1 1.4 %shard_map.102 = (bf16[256,1280]{1,0:T(8,128)(2,1)}, bf16[256,512]{1,0:T(8,128)(2,1)}, bf16[256,128]{1,0:T(8,128)(2,1)}, bf16[256,128]{1,0:T(8,128)(2,1)}, f32[512,640]{1,0:T(8,128)}) custom-call(bf16[256,1280]{1,0:T(8,128)(2,1)S(1)} %get-tuple-element.10.refs_0_, bf16[256,512]{1,0:T(8,128)(2,1)S(1)} %get-tuple-element.11.refs_1_, ...), custom_call_target="tpu_custom_call" | custom-call | tf_op jit(solution)/shard_map/pallas_call | solution.py:788

commit v5 on v4

--- a/solution.py
+++ b/solution.py
@@ -661,13 +661,13 @@
     layer_pair(spot)
     near(1, layer_begin)
     near(1, side_begin)
+    near(1, layer_pair)
+    near(1, up_block)
     near(0, up_block)
-    near(1, layer_pair)
     for distance in range(2, line - 1):
         heads_pass(distance, True)
         near(distance, side_begin)
-        near(distance - 1, up_block)
-    near(line - 2, up_block)
+        near(distance, up_block)
     near(line - 1, side_begin)
     near(line - 1, up_block)
     for distance in range(2, line):

time: 70.7 us -> 70.4 us (level)
  no operation moved by 1% of the time
where the time goes in v5:
time: 70.4 us; the launch traced here: 70.2 us
  Pallas kernels  69.6 us (99%)
    pallas_call x1, Pallas kernels, fused(): pl.pallas_call(functools.partial(branch_kernel, n_dp, n_mp), out_shape=(j...  68.1 us
    pallas_call x1, Pallas kernels, finish(): pl.pallas_call(finish_kernel, out_shape=tuple((jax.ShapeDtypeStruct(a.sha...  1.45 us

profile of v5, /device:TPU:6, one launch (start us, length us, event | category | flops | bytes accessed | tf_op | source)
XLA Modules:
  0.0 70.2 jit_solution(13069615233955339378)
XLA Ops:
  0.6 68.1 %shard_map.101 = (bf16[256,1280]{1,0:T(8,128)(2,1)S(1)}, bf16[256,512]{1,0:T(8,128)(2,1)S(1)}, bf16[256,128]{1,0:T(8,128)(2,1)S(1)}, bf16[256,128]{1,0:T(8,128)(2,1)S(1)}, f32[512,640]{1,0:T(8,128)S(1)}) custom-call(s32[1,8]{1,0:T(1,128)} %lengths_hbm.1, bf16[256,512]{1,0:T(8,128)(2,1)} %query_hbm.1, bf16[256,128]{1,0:T(8,128)(2,1)} %key_hbm.1, ...), custom_call_target="tpu_custom_call" | custom-call | tf_op jit(solution)/shard_map/pallas_call | solution.py:809
  68.8 1.4 %shard_map.102 = (bf16[256,1280]{1,0:T(8,128)(2,1)}, bf16[256,512]{1,0:T(8,128)(2,1)}, bf16[256,128]{1,0:T(8,128)(2,1)}, bf16[256,128]{1,0:T(8,128)(2,1)}, f32[512,640]{1,0:T(8,128)}) custom-call(bf16[256,1280]{1,0:T(8,128)(2,1)S(1)} %get-tuple-element.10.refs_0_, bf16[256,512]{1,0:T(8,128)(2,1)S(1)} %get-tuple-element.11.refs_1_, ...), custom_call_target="tpu_custom_call" | custom-call | tf_op jit(solution)/shard_map/pallas_call | solution.py:788
